TPU v7x, 32 devices: a whole 2x2x4 slice. The times are simulated.
32 devices in a mesh: prow: 8 (over z, y), pcol: 4 (over x, core).
Axes of the slice: x: 2, y: 2, z: 4, core: 2. Of those that a mesh axis runs over, the one named last changes fastest.
Arguments:
- iface_tiles: int32 [32, 16], replicated, may hold values from 0 to 63, as said below
- interior_sizes: int32 [32], P(('prow', 'pcol')), may hold values from 128 to 512
- coupling: float32 [32, 512, 2048], P(('prow', 'pcol')), may hold values from -0.25 to 0.25
- factor_inverse: float32 [32, 512, 512], P(('prow', 'pcol')), as said below
- interface_block: float32 [8, 8, 4, 16, 128, 128], P('prow', None, 'pcol'), as said below
Outputs:
- schur: float32 [8, 8, 4, 16, 128, 128], P('prow', None, 'pcol')
- panel: float32 [8, 8, 128, 128], P('prow', None, 'pcol')
Inputs may be any that keep to these rules, and one draw needn't show every extreme that they name: `iface_tiles`: each row holds 16 distinct tile numbers; for every r, exactly 2 of them are r modulo 8; every tile number stands in exactly 8 rows. `factor_inverse`: each matrix is lower triangular with a diagonal between 0.25 and 1. `interface_block`: diagonal entries lie between 80 and 160; other entries are of order one.
All inputs are finite; a program needn't handle non-finite values.
Results may differ from a plain program's by a relative error of at most 0.0001.
Values sent between devices are 32-bit elements; how exact they have to be, the bound alone decides.
A program may use at most 128 MiB of HBM per device.

v0:
```python
import functools

import jax
import jax.numpy as jnp
from jax import lax
from jax.experimental import pallas as pl
from jax.experimental.pallas import tpu as pltpu
from jax.sharding import Mesh, PartitionSpec as P

HIGHEST = lax.Precision.HIGHEST
MESH = pl.DeviceIdType.MESH


def split(x):
    high = x.astype(jnp.bfloat16)
    low = (x - high.astype(jnp.float32)).astype(jnp.bfloat16)
    return high, low


def dot3(a_high, a_low, b_high, b_low):
    dot = functools.partial(jnp.dot, preferred_element_type=jnp.float32)
    return dot(a_high, b_high) + (dot(a_high, b_low) + dot(a_low, b_high))


def members(tiles_ref, row, count, modulus, residue, want):
    found, places = [jnp.int32(0)] * want, [jnp.int32(0)] * want
    seen = jnp.int32(0)
    for j in range(count):
        tile = tiles_ref[row, j]
        match = lax.rem(tile, modulus) == residue
        for k in range(want):
            hit = match & (seen == k)
            found[k] = jnp.where(hit, tile, found[k])
            places[k] = jnp.where(hit, jnp.int32(j), places[k])
        seen = seen + match.astype(jnp.int32)
    return found, places


def factor_inverse_of(matrix):
    size = matrix.shape[0]
    rows = lax.broadcasted_iota(jnp.int32, matrix.shape, 0)
    cols = lax.broadcasted_iota(jnp.int32, matrix.shape, 1)

    def eliminate(j, carry):
        rest, inverse = carry
        row = jnp.sum(jnp.where(rows == j, rest, 0.0), axis=0, keepdims=True)
        column = jnp.sum(jnp.where(cols == j, rest, 0.0), axis=1, keepdims=True)
        pivot = jnp.sum(jnp.where(cols[:1] == j, row, 0.0), axis=1, keepdims=True)
        scale = 1.0 / jnp.sqrt(pivot)
        below = jnp.where(rows[:, :1] > j, column * scale, 0.0)
        solved = jnp.sum(jnp.where(rows == j, inverse, 0.0), axis=0, keepdims=True) * scale
        rest = rest - below * (row * scale)
        inverse = jnp.where(rows == j, solved, inverse - below * solved)
        return rest, inverse

    return lax.fori_loop(0, size, eliminate, (matrix, (rows == cols).astype(jnp.float32)))[1]


def exchange_kernel(
    halves, half_rows, cols_grid, rows_per, local_cols, width,
    tiles_ref, sizes_ref, coupling_ref, factor_ref, base_ref,
    own_ref, far_ref, inverse_ref, slots_ref,
    block_ref, square_ref, corner_ref, w_ref, across_ref, high_ref, low_ref, stage_ref, sums_ref, heard_ref,
    load_sem, across_send, across_recv, own_send, own_recv, far_send, far_recv, local_sem, sum_send, sum_recv,
):
    rows_grid = halves * half_rows
    group = half_rows * cols_grid
    laps = rows_grid // cols_grid
    iface = coupling_ref.shape[1]
    tile_count = iface // width
    block = rows_per * width
    half, sub, pcol = lax.axis_index("half"), lax.axis_index("sub"), lax.axis_index("pcol")
    prow = half * half_rows + sub
    me = sub * cols_grid + pcol
    self_index = half * group + me
    opposite = lax.rem(half + 1, halves)

    loads = [
        pltpu.make_async_copy(factor_ref, square_ref, load_sem.at[0]),
        pltpu.make_async_copy(base_ref.at[0], corner_ref, load_sem.at[1]),
    ]
    for j in range(tile_count):
        tile = coupling_ref.at[:, j * width : (j + 1) * width]
        loads.append(pltpu.make_async_copy(tile, block_ref.at[j], load_sem.at[2 + j]))
    for load in loads:
        load.start()

    def place(peer):
        return (half, peer // cols_grid, lax.rem(peer, cols_grid))

    barrier = pltpu.get_barrier_semaphore()

    def greet(k, carry):
        pl.semaphore_signal(barrier, inc=1, device_id=place(lax.rem(me + k, group)), device_id_type=MESH)
        return carry

    lax.fori_loop(1, group, greet, 0)
    pl.semaphore_signal(barrier, inc=1, device_id=(opposite, sub, pcol), device_id_type=MESH)

    order = []
    for m in range(rows_grid):
        order += members(tiles_ref, self_index, tile_count, rows_grid, m, rows_per)[1]
    first = jnp.int32(0)
    present = jnp.int32(0)
    for j in range(tile_count):
        hit = tiles_ref[self_index, j] == 0
        first = jnp.where(hit, jnp.int32(j), first)
        present = jnp.where(hit, jnp.int32(1), present)

    for load in loads:
        load.wait()
    factor_high, factor_low = split(square_ref[...])
    size = sizes_ref[0]

    def weigh(columns, limit):
        live = lax.broadcasted_iota(jnp.int32, columns.shape, 0) < limit
        product = dot3(factor_high, factor_low, *split(jnp.where(live, columns, 0.0)))
        return jnp.where(live, product, 0.0)

    product = weigh(block_ref[first], size * present)
    square = dot3(*split(product.T), *split(product))
    sums_ref[0] = jnp.where(self_index == 0, corner_ref[...], 0.0) - square

    def across_copy(m):
        return pltpu.make_async_remote_copy(
            src_ref=w_ref.at[m],
            dst_ref=across_ref.at[m],
            send_sem=across_send.at[m],
            recv_sem=across_recv.at[m],
            device_id=(opposite, sub, pcol),
            device_id_type=MESH,
        )

    for m in range(rows_grid):
        columns = jnp.concatenate([block_ref[at] for at in order[m * rows_per : (m + 1) * rows_per]], axis=1)
        product = weigh(columns, size)
        w_ref[m] = product
        high, low = split(product)
        high_ref[m] = high
        low_ref[m] = low
        if m == 0:
            pl.semaphore_wait(barrier, group)
        across_copy(m).start()

    def spread(source_ref, out_ref, send_sem, recv_sem):
        def copy_to(peer):
            return pltpu.make_async_remote_copy(
                src_ref=stage_ref.at[peer],
                dst_ref=out_ref.at[me],
                send_sem=send_sem.at[peer],
                recv_sem=recv_sem.at[me],
                device_id=place(peer),
                device_id_type=MESH,
            )

        def arriving(peer):
            return pltpu.make_async_remote_copy(
                src_ref=stage_ref.at[peer],
                dst_ref=out_ref.at[peer],
                send_sem=send_sem.at[peer],
                recv_sem=recv_sem.at[peer],
                device_id=place(peer),
                device_id_type=MESH,
            )

        def step(i, carry):
            target = lax.rem(sub + 1 + i, half_rows)
            row_high, row_low = split(source_ref[half * half_rows + target].T)
            for m in range(rows_grid):
                q, lap = m % cols_grid, m // cols_grid
                product = dot3(row_high, row_low, high_ref[m], low_ref[m])
                for r in range(rows_per):
                    for c in range(rows_per):
                        stage_ref[target * cols_grid + q, r, lap * rows_per + c] = product[
                            r * width : (r + 1) * width, c * width : (c + 1) * width
                        ]
            for shift in range(cols_grid):
                peer = target * cols_grid + lax.rem(pcol + shift, cols_grid)

                @pl.when(peer != me)
                def _():
                    copy_to(peer).start()

                @pl.when(peer == me)
                def _():
                    pltpu.make_async_copy(stage_ref.at[peer], out_ref.at[me], local_sem).start()

            return carry

        lax.fori_loop(0, half_rows, step, 0)

        def sent():
            pltpu.make_async_copy(stage_ref.at[me], out_ref.at[me], local_sem).wait()

            def wait(k, carry):
                copy_to(lax.rem(me + k, group)).wait_send()
                return carry

            lax.fori_loop(1, group, wait, 0)

        def arrived():
            def wait(k, carry):
                arriving(lax.rem(me + k, group)).wait_recv()
                return carry

            lax.fori_loop(1, group, wait, 0)

        return sent, arrived

    own_sent, own_arrived = spread(w_ref, own_ref, own_send, own_recv)

    steps = sums_ref.shape[0] - 1
    for k in range(steps):
        stride = 1 << (steps - 1 - k)
        peer = self_index ^ stride
        copy = pltpu.make_async_remote_copy(
            src_ref=sums_ref.at[k],
            dst_ref=heard_ref.at[k],
            send_sem=sum_send.at[k],
            recv_sem=sum_recv.at[k],
            device_id=(peer // group, lax.rem(peer, group) // cols_grid, lax.rem(peer, cols_grid)),
            device_id_type=MESH,
        )
        copy.start()
        copy.wait()
        sums_ref[k + 1] = sums_ref[k] + heard_ref[k]
    total = sums_ref[steps]
    inverse_ref[...] = factor_inverse_of(0.5 * (total + total.T))

    each = rows_per * laps * rows_per

    def place_tiles(n, carry):
        from_half = n // group
        sender = lax.rem(half + from_half, halves) * group + lax.rem(n, group)
        row_tiles = members(tiles_ref, sender, tile_count, rows_grid, prow, rows_per)[0]
        col_tiles = []
        for lap in range(laps):
            col_tiles += members(tiles_ref, sender, tile_count, rows_grid, lap * cols_grid + pcol, rows_per)[0]
        for r in range(rows_per):
            for c in range(laps * rows_per):
                slots_ref[n * each + r * laps * rows_per + c] = (
                    row_tiles[r] // rows_grid * local_cols
                    + col_tiles[c] // cols_grid
                )
        return carry

    lax.fori_loop(0, halves * group, place_tiles, 0)

    own_sent()
    for m in range(rows_grid):
        across_copy(m).wait()
        high, low = split(across_ref[m])
        high_ref[m] = high
        low_ref[m] = low
    far_sent, far_arrived = spread(across_ref, far_ref, far_send, far_recv)
    own_arrived()
    far_arrived()
    far_sent()


def exchange(tiles, sizes, coupling, factor, base, halves, half_rows, cols_grid, local_cols):
    interior, iface = coupling.shape
    width = base.shape[-1]
    rows_grid = halves * half_rows
    rows_per = iface // width // rows_grid
    cols_per = iface // width // cols_grid
    group = half_rows * cols_grid
    parts = (group, rows_per, cols_per, width, width)
    chunks = (rows_grid, interior, rows_per * width)
    steps = (halves * group).bit_length() - 1
    dma = pltpu.SemaphoreType.DMA
    anywhere = pl.BlockSpec(memory_space=pl.ANY)
    scalars = pl.BlockSpec(memory_space=pltpu.SMEM)
    return pl.pallas_call(
        functools.partial(exchange_kernel, halves, half_rows, cols_grid, rows_per, local_cols, width),
        in_specs=[scalars, scalars, anywhere, anywhere, anywhere],
        out_specs=[anywhere, anywhere, pl.BlockSpec(memory_space=pltpu.VMEM), scalars],
        out_shape=[
            jax.ShapeDtypeStruct(parts, jnp.float32),
            jax.ShapeDtypeStruct(parts, jnp.float32),
            jax.ShapeDtypeStruct((width, width), jnp.float32),
            jax.ShapeDtypeStruct((halves * group * rows_per * cols_per,), jnp.int32),
        ],
        scratch_shapes=[
            pltpu.VMEM((iface // width, interior, width), jnp.float32),
            pltpu.VMEM((interior, interior), jnp.float32),
            pltpu.VMEM((width, width), jnp.float32),
            pltpu.VMEM(chunks, jnp.float32),
            pltpu.VMEM(chunks, jnp.float32),
            pltpu.VMEM(chunks, jnp.bfloat16),
            pltpu.VMEM(chunks, jnp.bfloat16),
            pltpu.VMEM(parts, jnp.float32),
            pltpu.VMEM((steps + 1, width, width), jnp.float32),
            pltpu.VMEM((steps, width, width), jnp.float32),
            dma((iface // width + 2,)),
            dma((rows_grid,)), dma((rows_grid,)),
            dma((group,)), dma((group,)),
            dma((group,)), dma((group,)),
            dma,
            dma((steps,)), dma((steps,)),
        ],
        compiler_params=pltpu.CompilerParams(
            vmem_limit_bytes=40 << 20, collective_id=0, has_side_effects=True
        ),
        name="exchange",
    )(tiles, sizes, coupling, factor, base)


def subtract_kernel(slots_ref, base_ref, own_ref, far_ref, out_ref, sum_ref, load_sem, store_sem):
    load = pltpu.make_async_copy(base_ref, sum_ref, load_sem)
    load.start()
    load.wait()
    senders, count = own_ref.shape[:2]
    for shift, parts_ref in enumerate((own_ref, far_ref)):

        def take(n, carry):
            for i in range(count):
                slot = slots_ref[(shift * senders + n) * count + i]
                sum_ref[slot] = sum_ref[slot] - parts_ref[n, i]
            return carry

        lax.fori_loop(0, senders, take, 0)
    store = pltpu.make_async_copy(sum_ref, out_ref, store_sem)
    store.start()
    store.wait()


def subtract(slots, base, own, far):
    vmem = pl.BlockSpec(memory_space=pltpu.VMEM)
    anywhere = pl.BlockSpec(memory_space=pl.ANY)
    return pl.pallas_call(
        subtract_kernel,
        in_specs=[pl.BlockSpec(memory_space=pltpu.SMEM), anywhere, vmem, vmem],
        out_specs=anywhere,
        out_shape=jax.ShapeDtypeStruct(base.shape, jnp.float32),
        scratch_shapes=[
            pltpu.VMEM(base.shape, jnp.float32),
            pltpu.SemaphoreType.DMA,
            pltpu.SemaphoreType.DMA,
        ],
        compiler_params=pltpu.CompilerParams(vmem_limit_bytes=44 << 20),
        cost_estimate=pl.CostEstimate(
            flops=own.size + far.size, bytes_accessed=8 * own.size + 8 * base.size, transcendentals=0
        ),
        name="subtract",
    )(slots, base, own, far)


def shards(iface_tiles, interior_sizes, coupling, factor_inverse, interface_block):
    halves, half_rows = lax.axis_size("half"), lax.axis_size("sub")
    cols_grid = lax.axis_size("pcol")
    pcol_index = lax.axis_index("pcol")
    width = interface_block.shape[-1]
    local_rows, local_cols = interface_block.shape[1], interface_block.shape[3]
    share = width // cols_grid
    group = half_rows * cols_grid

    base = interface_block.reshape(local_rows * local_cols, width, width)
    own, far, inverse, slots = exchange(
        iface_tiles, interior_sizes, coupling[0], factor_inverse[0], base, halves, half_rows, cols_grid, local_cols
    )
    summed = subtract(
        slots, base, own.reshape(group, -1, width, width), far.reshape(group, -1, width, width)
    )
    schur = summed.reshape(interface_block.shape)

    column = summed.reshape(local_rows, local_cols, width, width)[:, 0]
    kept = jnp.where(pcol_index == 0, column[:, :share], 0.0)
    for q in range(1, cols_grid):
        kept = kept + lax.ppermute(column[:, q * share : (q + 1) * share], "pcol", [(0, q)])
    panel = jnp.einsum("atu,vu->atv", kept, inverse, precision=HIGHEST)
    return (schur, panel[None])


def solution(mesh):
    rows_grid, cols_grid = mesh.shape["prow"], mesh.shape["pcol"]
    grid = Mesh(
        mesh.devices.reshape(2, rows_grid // 2, cols_grid), ("half", "sub", "pcol")
    )
    prow = ("half", "sub")
    every = ("half", "sub", "pcol")
    in_specs = (
        P(),
        P(every),
        P(every, None, None),
        P(every, None, None),
        P(prow, None, "pcol", None, None, None),
    )
    out_specs = (P(prow, None, "pcol", None, None, None), P(prow, None, "pcol", None))
    return jax.shard_map(shards, mesh=grid, in_specs=in_specs, out_specs=out_specs, check_vma=False)
```

profile of v0, /device:TPU:7, one launch (start us, length us, event | category | flops | bytes accessed | tf_op | source)
XLA Modules:
  0.0 382.5 jit_solution(6311661993949505989)
XLA Ops:
  0.6 0.8 copy.7.tiles_ref
  1.4 0.0 copy-start
  2.2 0.0 copy-start.2
  2.2 2.3 copy-done.2
  4.5 0.0 copy-start.3
  4.5 1.6 copy-done.3
  6.1 351.2 %exchange.1 = (f32[16,2,4,128,128]{4,3,2,1,0:T(8,128)S(1)}, f32[16,2,4,128,128]{4,3,2,1,0:T(8,128)}, f32[128,128]{1,0:T(8,128)S(1)}, s32[256]{0:T(256)S(1)}) custom-call(s32[32,16]{1,0:T(8,128)S(1)} %copy.7.tiles_ref, s32[1]{0:T(128)S(6)} %copy.11.sizes_ref, f32[512,2048]{1,0:T(8,128)S(1)} %bitcast.21, f32[512,512]{1,0:T(8,128)S(1)} %bitcast.22, ...), custom_call_target="tpu_custom_call" | custom-call | tf_op jit(solution)/shard_map/exchange/pallas_call | solution.py:274
  357.4 0.0 copy-start.1
  357.4 3.2 copy-done.1
  360.6 0.0 copy-done
  360.6 11.7 %subtract.1 = f32[128,128,128]{2,1,0:T(8,128)} custom-call(s32[256]{0:T(256)S(1)} %get-tuple-element.6.slots_ref, f32[128,128,128]{2,1,0:T(8,128)S(1)} %bitcast.19, f32[16,8,128,128]{3,2,1,0:T(8,128)} %bitcast.20, f32[16,8,128,128]{3,2,1,0:T(8,128)} %bitcast.25), custom_call_target="tpu_custom_call" | custom-call | flops 4194304 | bytes 33554432 | tf_op jit(solution)/shard_map/subtract/pallas_call | solution.py:331
  372.3 1.1 slice_bitcast_fusion
  373.4 0.7 collective-permute-start
  374.1 0.7 collective-permute-start.1
  374.7 1.3 collective-permute-start.2
  376.0 0.0 collective-permute-done
  376.1 0.0 collective-permute-done.1
  376.1 5.5 %collective-permute-done.2 = f32[8,32,128]{2,1,0:T(8,128)S(1)} collective-permute-done((f32[8,32,128]{2,1,0:T(8,128)S(1)}, f32[8,32,128]{2,1,0:T(8,128)S(1)}, u32[]{:S(2)}, u32[]{:S(2)}) %collective-permute-start.2) | collective-permute-done | bytes 131104 | tf_op jit(solution)/shard_map/ppermute | solution.py:370
  381.5 0.9 convolution_bitcast_fusion
  (1 shorter events, 0.0 us)
Async XLA Ops:
  1.4 359.2 %copy-start = (f32[1,8,1,16,128,128]{5,4,3,2,1,0:T(8,128)S(1)}, f32[1,8,1,16,128,128]{5,4,3,2,1,0:T(8,128)}, u32[]{:S(2)}) copy-start(f32[1,8,1,16,128,128]{5,4,3,2,1,0:T(8,128)} %param.9) | copy-start | bytes 25165828
  2.2 2.3 copy-start.2
  4.5 1.6 copy-start.3
  357.4 3.2 copy-start.1
  373.4 2.7 collective-permute-start
  374.1 2.0 collective-permute-start.1
  374.7 6.8 %collective-permute-start.2 = (f32[8,32,128]{2,1,0:T(8,128)S(1)}, f32[8,32,128]{2,1,0:T(8,128)S(1)}, u32[]{:S(2)}, u32[]{:S(2)}) collective-permute-start(f32[8,32,128]{2,1,0:T(8,128)S(1)} %get-tuple-element.13), channel_id=1, source_target_pairs={{0,3},{4,7},{8,11},{12,15},{16,19},{20,23},{24,27},{28,31}} | collective-permute-start | bytes 393224 | tf_op jit(solution)/shard_map/ppermute | solution.py:370
where the time goes:
time: 384 us; the launch traced here: 382 us
  Pallas kernels  363 us (95%)
  local copies, waits for them, and re-layouts  9.01 us (2%)
  waiting for transfers between devices  5.47 us (1%)
    pallas_call x1, Pallas kernels, exchange(): pl.pallas_call(functools.partial(exchange_kernel, halves, half_rows, cols...  351 us
    pallas_call x1, Pallas kernels, subtract(): pl.pallas_call(subtract_kernel, in_specs=[pl.BlockSpec(memory_space=pltpu...  11.7 us
    unnamed x9, local copies, waits for them, and re-layouts  7.9 us
  transfers between devices with their start and end apart: 3, of which 1 were waited for; matrix products, arithmetic and copies ran while one was open for 0% of the time, Pallas kernels for 0%

commit v1 on v0

v1 whole, which is shorter than its diff:
```python
import functools

import jax
import jax.numpy as jnp
from jax import lax
from jax.experimental import pallas as pl
from jax.experimental.pallas import tpu as pltpu
from jax.sharding import Mesh, PartitionSpec as P

HIGHEST = lax.Precision.HIGHEST
MESH = pl.DeviceIdType.MESH
LAYERS = 4


def split(x):
    high = x.astype(jnp.bfloat16)
    low = (x - high.astype(jnp.float32)).astype(jnp.bfloat16)
    return high, low


def dot3(a_high, a_low, b_high, b_low):
    dot = functools.partial(jnp.dot, preferred_element_type=jnp.float32)
    return dot(a_high, b_high) + (dot(a_high, b_low) + dot(a_low, b_high))


def members(tiles_ref, row, count, modulus, residue, want):
    found, places = [jnp.int32(0)] * want, [jnp.int32(0)] * want
    seen = jnp.int32(0)
    for j in range(count):
        tile = tiles_ref[row, j]
        match = lax.rem(tile, modulus) == residue
        for k in range(want):
            hit = match & (seen == k)
            found[k] = jnp.where(hit, tile, found[k])
            places[k] = jnp.where(hit, jnp.int32(j), places[k])
        seen = seen + match.astype(jnp.int32)
    return found, places


def factor_inverse_of(matrix):
    size = matrix.shape[0]
    rows = lax.broadcasted_iota(jnp.int32, matrix.shape, 0)
    cols = lax.broadcasted_iota(jnp.int32, matrix.shape, 1)

    def eliminate(j, carry):
        rest, inverse = carry
        row = jnp.sum(jnp.where(rows == j, rest, 0.0), axis=0, keepdims=True)
        column = jnp.sum(jnp.where(cols == j, rest, 0.0), axis=1, keepdims=True)
        pivot = jnp.sum(jnp.where(cols[:1] == j, row, 0.0), axis=1, keepdims=True)
        scale = 1.0 / jnp.sqrt(pivot)
        below = jnp.where(rows[:, :1] > j, column * scale, 0.0)
        solved = jnp.sum(jnp.where(rows == j, inverse, 0.0), axis=0, keepdims=True) * scale
        rest = rest - below * (row * scale)
        inverse = jnp.where(rows == j, solved, inverse - below * solved)
        return rest, inverse

    return lax.fori_loop(0, size, eliminate, (matrix, (rows == cols).astype(jnp.float32)))[1]


def exchange_kernel(
    layers, layer_rows, cols_grid, rows_per, local_cols, width,
    tiles_ref, sizes_ref, coupling_ref, factor_ref, base_ref,
    parts_ref, start_ref, inverse_ref, slots_ref,
    block_ref, square_ref, corner_ref, w_ref, high_ref, low_ref, row_high_ref, row_low_ref, stage_ref, sums_ref, heard_ref,
    load_sem, base_sem, up_send, down_send, arrive, tile_send, tile_recv, sum_send, sum_recv,
):
    classes = layers * layer_rows
    group = layer_rows * cols_grid
    laps = classes // cols_grid
    tile_count = block_ref.shape[0]
    layer, sub, pcol = lax.axis_index("layer"), lax.axis_index("sub"), lax.axis_index("pcol")
    me = sub * cols_grid + pcol
    self_index = layer * group + me
    prow = layer * layer_rows + sub
    last = layers - 1

    loads = [
        pltpu.make_async_copy(factor_ref, square_ref, load_sem.at[0]),
        pltpu.make_async_copy(base_ref.at[0], corner_ref, load_sem.at[1]),
    ]
    for j in range(tile_count):
        tile = coupling_ref.at[:, j * width : (j + 1) * width]
        loads.append(pltpu.make_async_copy(tile, block_ref.at[j], load_sem.at[2 + j]))
    for load in loads:
        load.start()
    preload = pltpu.make_async_copy(base_ref, start_ref, base_sem)
    preload.start()

    barrier = pltpu.get_barrier_semaphore()

    def greet(k, carry):
        peer = lax.rem(me + k, group)
        pl.semaphore_signal(
            barrier, inc=1, device_id=(layer, peer // cols_grid, lax.rem(peer, cols_grid)), device_id_type=MESH
        )
        return carry

    lax.fori_loop(1, group, greet, 0)
    for other in (last - layer, layer ^ 1):
        pl.semaphore_signal(barrier, inc=1, device_id=(other, sub, pcol), device_id_type=MESH)

    first = jnp.int32(0)
    present = jnp.int32(0)
    for j in range(tile_count):
        hit = tiles_ref[self_index, j] == 0
        first = jnp.where(hit, jnp.int32(j), first)
        present = jnp.where(hit, jnp.int32(1), present)

    for load in loads:
        load.wait()
    factor_high, factor_low = split(square_ref[...])
    size = sizes_ref[0]

    def weigh(columns, limit):
        live = lax.broadcasted_iota(jnp.int32, columns.shape, 0) < limit
        product = dot3(factor_high, factor_low, *split(jnp.where(live, columns, 0.0)))
        return jnp.where(live, product, 0.0)

    product = weigh(block_ref[first], size * present)
    square = dot3(*split(product.T), *split(product))
    sums_ref[0] = jnp.where(self_index == 0, corner_ref[...], 0.0) - square

    def up_copy(source, m):
        return pltpu.make_async_remote_copy(
            src_ref=w_ref.at[source, m],
            dst_ref=w_ref.at[source, m],
            send_sem=up_send.at[source, m],
            recv_sem=arrive.at[source, m],
            device_id=(jnp.minimum(layer + 1, last), sub, pcol),
            device_id_type=MESH,
        )

    def down_copy(source, m):
        return pltpu.make_async_remote_copy(
            src_ref=w_ref.at[source, m],
            dst_ref=w_ref.at[source, m],
            send_sem=down_send.at[source, m],
            recv_sem=arrive.at[source, m],
            device_id=(jnp.maximum(layer - 1, 0), sub, pcol),
            device_id_type=MESH,
        )

    def pass_up(source, m):
        @pl.when(layer < last)
        def _():
            up_copy(source, m).start()

    def pass_down(source, m):
        @pl.when(layer > 0)
        def _():
            down_copy(source, m).start()

    steps = sums_ref.shape[0] - 1

    def sum_copy(k):
        if k == 0:
            partner = (last - layer, sub, pcol)
        elif k == 1:
            partner = (layer ^ 1, sub, pcol)
        else:
            peer = me ^ (group >> (k - 1))
            partner = (layer, peer // cols_grid, lax.rem(peer, cols_grid))
        return pltpu.make_async_remote_copy(
            src_ref=sums_ref.at[k],
            dst_ref=heard_ref.at[k],
            send_sem=sum_send.at[k],
            recv_sem=sum_recv.at[k],
            device_id=partner,
            device_id_type=MESH,
        )

    def sum_up(k):
        sum_copy(k).wait()
        sums_ref[k + 1] = sums_ref[k] + heard_ref[k]

    def keep(m, product):
        high, low = split(product)
        high_ref[m] = high
        low_ref[m] = low

    def weigh_class(m):
        order = members(tiles_ref, self_index, tile_count, classes, m, rows_per)[1]
        product = weigh(jnp.concatenate([block_ref[at] for at in order], axis=1), size)
        w_ref[layer, m] = product
        keep(m, product)

    pl.semaphore_wait(barrier, group + 1)
    sum_copy(0).start()
    weigh_class(0)
    sum_up(0)
    sum_copy(1).start()
    weigh_class(last * layer_rows)
    sum_up(1)
    sum_copy(2).start()
    for m in (0, last * layer_rows):
        pass_up(layer, m)
        pass_down(layer, m)

    def weigh_rest(m, carry):
        @pl.when((m != 0) & (m != last * layer_rows))
        def _():
            weigh_class(m)
            pass_up(layer, m)
            pass_down(layer, m)

        return carry

    lax.fori_loop(0, classes, weigh_rest, 0)
    for k in range(2, steps):
        sum_up(k)
        if k + 1 < steps:
            sum_copy(k + 1).start()

    def tiles_out(source, m, slot, target):
        q, lap = lax.rem(m, cols_grid), m // cols_grid
        return pltpu.make_async_remote_copy(
            src_ref=stage_ref.at[slot, m, target],
            dst_ref=parts_ref.at[source * group + me, lap],
            send_sem=tile_send.at[slot, m, target],
            recv_sem=tile_recv.at[source * group + me, lap],
            device_id=(layer, target, q),
            device_id_type=MESH,
        )

    def take_rows(source):
        for t in range(layer_rows):
            high, low = split(w_ref[source, layer * layer_rows + t].T)
            row_high_ref[t] = high
            row_low_ref[t] = low

    def column(source, m, slot):
        q, lap = lax.rem(m, cols_grid), m // cols_grid
        for t in range(layer_rows):
            product = dot3(row_high_ref[t], row_low_ref[t], high_ref[m], low_ref[m])
            away = (q != pcol) | (sub != t)

            def write(ref):
                for r in range(rows_per):
                    for c in range(rows_per):
                        ref[r, c] = product[r * width : (r + 1) * width, c * width : (c + 1) * width]

            @pl.when(away)
            def _():
                write(stage_ref.at[slot, m, t])
                tiles_out(source, m, slot, t).start()

            @pl.when(jnp.logical_not(away))
            def _():
                write(parts_ref.at[source * group + me, lap])

    def sent(source, slot):
        def wait(n, carry):
            m, t = n // layer_rows, lax.rem(n, layer_rows)

            @pl.when((lax.rem(m, cols_grid) != pcol) | (sub != t))
            def _():
                tiles_out(source, m, slot, t).wait_send()

            return carry

        lax.fori_loop(0, classes * layer_rows, wait, 0)

    def columns(source, slot, ordered, low, top):
        def step(i, carry):
            column(source, ordered(i), slot)
            return carry

        lax.fori_loop(low, top, step, 0)

    def straight(i):
        return i

    middle = classes // 2

    def up_order(i):
        near_end = classes - layer_rows * (1 + i // layer_rows) + lax.rem(i, layer_rows)
        return jnp.where(i < middle, near_end, lax.rem(i + 1 + pcol, middle))

    def down_order(i):
        return jnp.where(i < middle, i, middle + lax.rem(i + 1 + pcol, middle))

    take_rows(layer)
    columns(layer, 0, straight, 0, classes)

    total = sums_ref[steps]
    inverse_ref[...] = factor_inverse_of(0.5 * (total + total.T))

    each = rows_per * laps * rows_per

    def place_tiles(sender, carry):
        row_tiles = members(tiles_ref, sender, tile_count, classes, prow, rows_per)[0]
        for lap in range(laps):
            col_tiles = members(tiles_ref, sender, tile_count, classes, lap * cols_grid + pcol, rows_per)[0]
            for r in range(rows_per):
                for c in range(rows_per):
                    slots_ref[sender * each + (lap * rows_per + r) * rows_per + c] = (
                        row_tiles[r] // classes * local_cols + col_tiles[c] // cols_grid
                    )
        return carry

    def relay(i, carry):
        @pl.when(layer > 0)
        def _():
            source, m = layer - 1, up_order(i)
            up_copy(source, m).wait_recv()
            pass_up(source, m)

        @pl.when(layer < last)
        def _():
            source, m = layer + 1, down_order(i)
            down_copy(source, m).wait_recv()
            pass_down(source, m)

        return carry

    lax.fori_loop(0, classes, relay, 0)

    def absorb(source, slot):
        def prepare(m, carry):
            keep(m, w_ref[source, m])
            return carry

        lax.fori_loop(0, classes, prepare, 0)
        take_rows(source)
        columns(source, slot, straight, 0, classes)

    @pl.when(layer > 0)
    def _():
        absorb(layer - 1, 1)

    sent(layer, 0)

    @pl.when(layer < last)
    def _():
        absorb(layer + 1, 0)

    @pl.when(layer > 0)
    def _():
        sent(layer - 1, 1)

    rising = layer >= layers // 2

    def order(i):
        return jnp.where(rising, up_order(i), down_order(i))

    def stream(distance, slot, passing):
        source = jnp.where(rising, layer - distance, layer + distance)

        def receive(i):
            m = order(i)
            up_copy(source, m).wait_recv()
            if passing:

                @pl.when(rising)
                def _():
                    pass_up(source, m)

                @pl.when(jnp.logical_not(rising))
                def _():
                    pass_down(source, m)

            keep(m, w_ref[source, m])
            return m

        def gather(i, carry):
            receive(i)
            return carry

        lax.fori_loop(0, middle, gather, 0)
        take_rows(source)
        columns(source, slot, order, 0, middle)

        def step(i, carry):
            column(source, receive(i), slot)
            return carry

        lax.fori_loop(middle, classes, step, 0)

    stream(2, 1, True)
    lax.fori_loop(0, layers * group, place_tiles, 0)

    @pl.when(layer < last)
    def _():
        sent(layer + 1, 0)

    ends = (layer == 0) | (layer == last)

    @pl.when(ends)
    def _():
        stream(3, 0, False)

    def landed(n, carry):
        source, k = n // group, lax.rem(n, group)

        @pl.when(k > 0)
        def _():
            peer = lax.rem(me + k, group)
            for lap in range(laps):
                pltpu.make_async_remote_copy(
                    src_ref=stage_ref.at[0, 0, 0],
                    dst_ref=parts_ref.at[source * group + peer, lap],
                    send_sem=tile_send.at[0, 0, 0],
                    recv_sem=tile_recv.at[source * group + peer, lap],
                    device_id=(layer, peer // cols_grid, lax.rem(peer, cols_grid)),
                    device_id_type=MESH,
                ).wait_recv()

        return carry

    lax.fori_loop(0, layers * group, landed, 0)
    sent(jnp.where(rising, layer - 2, layer + 2), 1)

    @pl.when(ends)
    def _():
        sent(jnp.where(rising, layer - 3, layer + 3), 0)

    def passed(source, carry):
        def wait(m, inner):
            @pl.when((source <= layer) & (layer < last))
            def _():
                up_copy(source, m).wait_send()

            @pl.when((source >= layer) & (layer > 0))
            def _():
                down_copy(source, m).wait_send()

            return inner

        return lax.fori_loop(0, classes, wait, carry)

    lax.fori_loop(0, layers, passed, 0)
    preload.wait()


def exchange(tiles, sizes, coupling, factor, base, layers, layer_rows, cols_grid, local_cols):
    interior, iface = coupling.shape
    width = base.shape[-1]
    classes = layers * layer_rows
    rows_per = iface // width // classes
    laps = classes // cols_grid
    group = layer_rows * cols_grid
    senders = layers * group
    parts = (senders, laps, rows_per, rows_per, width, width)
    chunks = (classes, interior, rows_per * width)
    steps = senders.bit_length() - 1
    dma = pltpu.SemaphoreType.DMA
    vmem = pl.BlockSpec(memory_space=pltpu.VMEM)
    hbm = pl.BlockSpec(memory_space=pltpu.HBM)
    scalars = pl.BlockSpec(memory_space=pltpu.SMEM)
    return pl.pallas_call(
        functools.partial(exchange_kernel, layers, layer_rows, cols_grid, rows_per, local_cols, width),
        in_specs=[scalars, scalars, hbm, hbm, hbm],
        out_specs=[vmem, vmem, vmem, scalars],
        out_shape=[
            pltpu.VMEM(parts, jnp.float32),
            pltpu.VMEM(base.shape, jnp.float32),
            jax.ShapeDtypeStruct((width, width), jnp.float32),
            jax.ShapeDtypeStruct((senders * laps * rows_per * rows_per,), jnp.int32),
        ],
        scratch_shapes=[
            pltpu.VMEM((iface // width, interior, width), jnp.float32),
            pltpu.VMEM((interior, interior), jnp.float32),
            pltpu.VMEM((width, width), jnp.float32),
            pltpu.VMEM((layers, *chunks), jnp.float32),
            pltpu.VMEM(chunks, jnp.bfloat16),
            pltpu.VMEM(chunks, jnp.bfloat16),
            pltpu.VMEM((layer_rows, rows_per * width, interior), jnp.bfloat16),
            pltpu.VMEM((layer_rows, rows_per * width, interior), jnp.bfloat16),
            pltpu.VMEM((2, classes, layer_rows, rows_per, rows_per, width, width), jnp.float32),
            pltpu.VMEM((steps + 1, width, width), jnp.float32),
            pltpu.VMEM((steps, width, width), jnp.float32),
            dma((iface // width + 2,)), dma,
            dma((layers, classes)), dma((layers, classes)), dma((layers, classes)),
            dma((2, classes, layer_rows)), dma((senders, laps)),
            dma((steps,)), dma((steps,)),
        ],
        compiler_params=pltpu.CompilerParams(
            vmem_limit_bytes=38 << 20, collective_id=0, has_side_effects=True
        ),
        name="exchange",
    )(tiles, sizes, *(pltpu.with_memory_space_constraint(x, pltpu.HBM) for x in (coupling, factor, base)))


def subtract_kernel(slots_ref, start_ref, parts_ref, out_ref, sum_ref, store_sem):
    senders, count = parts_ref.shape[:2]

    def take(n, carry):
        for i in range(count):
            slot = slots_ref[n * count + i]
            sum_ref[slot] = sum_ref[slot] - parts_ref[n, i]
        return carry

    lax.fori_loop(0, senders, take, 0)
    store = pltpu.make_async_copy(sum_ref, out_ref, store_sem)
    store.start()
    store.wait()


def subtract(slots, start, parts):
    vmem = pl.BlockSpec(memory_space=pltpu.VMEM)
    return pl.pallas_call(
        subtract_kernel,
        in_specs=[pl.BlockSpec(memory_space=pltpu.SMEM), vmem, vmem],
        out_specs=[pl.BlockSpec(memory_space=pltpu.HBM), vmem],
        out_shape=[pltpu.HBM(start.shape, jnp.float32), pltpu.VMEM(start.shape, jnp.float32)],
        input_output_aliases={1: 1},
        scratch_shapes=[pltpu.SemaphoreType.DMA],
        compiler_params=pltpu.CompilerParams(vmem_limit_bytes=1 << 20),
        cost_estimate=pl.CostEstimate(
            flops=parts.size, bytes_accessed=8 * parts.size + 4 * start.size, transcendentals=0
        ),
        name="subtract",
    )(slots, start, parts)


def shards(iface_tiles, interior_sizes, coupling, factor_inverse, interface_block):
    layers, layer_rows = lax.axis_size("layer"), lax.axis_size("sub")
    cols_grid = lax.axis_size("pcol")
    pcol_index = lax.axis_index("pcol")
    width = interface_block.shape[-1]
    local_rows, local_cols = interface_block.shape[1], interface_block.shape[3]
    share = width // cols_grid

    base = interface_block.reshape(local_rows * local_cols, width, width)
    parts, start, inverse, slots = exchange(
        iface_tiles, interior_sizes, coupling[0], factor_inverse[0], base, layers, layer_rows, cols_grid, local_cols
    )
    summed, kept_tiles = subtract(slots, start, parts.reshape(parts.shape[0], -1, width, width))
    schur = summed.reshape(interface_block.shape)

    column = kept_tiles.reshape(local_rows, local_cols, width, width)[:, 0]
    kept = jnp.where(pcol_index == 0, column[:, :share], 0.0)
    for q in range(1, cols_grid):
        kept = kept + lax.ppermute(column[:, q * share : (q + 1) * share], "pcol", [(0, q)])
    panel = jnp.einsum("atu,vu->atv", kept, inverse, precision=HIGHEST)
    return (schur, panel[None])


def solution(mesh):
    rows_grid, cols_grid = mesh.shape["prow"], mesh.shape["pcol"]
    grid = Mesh(
        mesh.devices.reshape(LAYERS, rows_grid // LAYERS, cols_grid), ("layer", "sub", "pcol")
    )
    prow = ("layer", "sub")
    every = ("layer", "sub", "pcol")
    in_specs = (
        P(),
        P(every),
        P(every, None, None),
        P(every, None, None),
        P(prow, None, "pcol", None, None, None),
    )
    out_specs = (P(prow, None, "pcol", None, None, None), P(prow, None, "pcol", None))
    return jax.shard_map(shards, mesh=grid, in_specs=in_specs, out_specs=out_specs, check_vma=False)
```

time: 384 us -> 314 us (0.82)
  Pallas kernels: 363 us -> 299 us
  local copies, waits for them, and re-layouts: 9.01 us -> 2.1 us
    pallas_call x1, Pallas kernels: 351 us -> 293 us  [exchange(): pl.pallas_call(functools.partial(exchange_kernel, layers, layer_rows, col...]
    unnamed x9 -> x5, local copies, waits for them, and re-layouts: 7.9 us -> 2.04 us
    pallas_call x1, Pallas kernels: 11.7 us -> 6.07 us  [subtract(): pl.pallas_call(subtract_kernel, in_specs=[pl.BlockSpec(memory_space=pltpu...]
where the time goes in v1:
time: 314 us; the launch traced here: 313 us
  Pallas kernels  299 us (95%)
  waiting for transfers between devices  7.53 us (2%)
    pallas_call x1, Pallas kernels, exchange(): pl.pallas_call(functools.partial(exchange_kernel, layers, layer_rows, col...  293 us
    ppermute x3, waiting for transfers between devices, shards(): lax.ppermute(column[:, q * share:(q + 1) * share], 'pcol', [(0, q)])  7.53 us
  transfers between devices with their start and end apart: 3, of which 1 were waited for; matrix products, arithmetic and copies ran while one was open for 0% of the time, Pallas kernels for 0%

profile of v1, /device:TPU:7, one launch (start us, length us, event | category | flops | bytes accessed | tf_op | source)
XLA Modules:
  0.0 313.4 jit_solution(415522166121407697)
XLA Ops:
  0.6 1.4 copy.8.tiles_ref
  2.7 292.7 %exchange.1 = (f32[32,2,2,2,128,128]{5,4,3,2,1,0:T(8,128)S(1)}, f32[128,128,128]{2,1,0:T(8,128)S(1)}, f32[128,128]{1,0:T(8,128)}, s32[256]{0:T(256)}) custom-call(s32[32,16]{1,0:T(8,128)} %copy.8.tiles_ref, s32[1]{0:T(128)S(6)} %copy.13.sizes_ref, f32[512,2048]{1,0:T(8,128)} %bitcast.20, f32[512,512]{1,0:T(8,128)} %bitcast.21, f32[128,128,128]{2,1,0:T(8,128)} %bitcast.19), custom_call_target="tpu_custom_call" | custom-call | tf_op jit(solution)/shard_map/exchange/pallas_call | solution.py:450
  295.4 0.0 copy-start
  295.4 0.7 copy-done
  296.1 0.0 copy-start.1
  296.1 6.1 %subtract.1 = (f32[128,128,128]{2,1,0:T(8,128)}, f32[128,128,128]{2,1,0:T(8,128)S(1)}) custom-call(s32[256]{0:T(256)S(1)} %copy-done, f32[128,128,128]{2,1,0:T(8,128)S(1)} %get-tuple-element.9.start_ref, f32[32,8,128,128]{3,2,1,0:T(8,128)S(1)} %bitcast.17), custom_call_target="tpu_custom_call", output_to_operand_aliasing={{1}: (1, {})} | custom-call | flops 4194304 | bytes 41943040 | tf_op jit(solution)/shard_map/subtract/pallas_call | solution.py:501
  302.2 0.7 collective-permute-start
  302.9 0.7 collective-permute-start.1
  303.6 1.3 collective-permute-start.2
  304.9 0.0 collective-permute-done
  304.9 0.0 collective-permute-done.1
  304.9 7.5 %collective-permute-done.2 = f32[8,32,128]{2,1,0:T(8,128)S(1)} collective-permute-done((f32[8,32,128]{2,1,0:T(8,128)S(1)}, f32[8,32,128]{2,1,0:T(8,128)S(1)}, u32[]{:S(2)}, u32[]{:S(2)}) %collective-permute-start.2) | collective-permute-done | bytes 131104 | tf_op jit(solution)/shard_map/ppermute | solution.py:534
  312.4 0.0 copy-done.1
  312.4 0.9 convolution_bitcast_fusion
  (2 shorter events, 0.1 us)
Async XLA Ops:
  295.4 0.7 copy-start
  296.1 16.4 %copy-start.1 = (f32[128,128]{1,0:T(8,128)S(1)}, f32[128,128]{1,0:T(8,128)}, u32[]{:S(2)}) copy-start(f32[128,128]{1,0:T(8,128)} %get-tuple-element.13) | copy-start | bytes 196612
  302.2 2.7 collective-permute-start
  302.9 2.0 collective-permute-start.1
  303.6 8.9 %collective-permute-start.2 = (f32[8,32,128]{2,1,0:T(8,128)S(1)}, f32[8,32,128]{2,1,0:T(8,128)S(1)}, u32[]{:S(2)}, u32[]{:S(2)}) collective-permute-start(f32[8,32,128]{2,1,0:T(8,128)S(1)} %get-tuple-element.17), channel_id=1, source_target_pairs={{0,3},{4,7},{8,11},{12,15},{16,19},{20,23},{24,27},{28,31}} | collective-permute-start | bytes 393224 | tf_op jit(solution)/shard_map/ppermute | solution.py:534

commit v2 on v1

v2 whole, which is shorter than its diff:
```python
import functools

import jax
import jax.numpy as jnp
from jax import lax
from jax.experimental import pallas as pl
from jax.experimental.pallas import tpu as pltpu
from jax.sharding import Mesh, PartitionSpec as P

HIGHEST = lax.Precision.HIGHEST
MESH = pl.DeviceIdType.MESH
LAYERS = 4


def split(x):
    high = x.astype(jnp.bfloat16)
    low = (x - high.astype(jnp.float32)).astype(jnp.bfloat16)
    return high, low


def dot3(a_high, a_low, b_high, b_low):
    dot = functools.partial(jnp.dot, preferred_element_type=jnp.float32)
    return dot(a_high, b_high) + (dot(a_high, b_low) + dot(a_low, b_high))


def members(tiles_ref, row, count, modulus, residue, want):
    found, places = [jnp.int32(0)] * want, [jnp.int32(0)] * want
    seen = jnp.int32(0)
    for j in range(count):
        tile = tiles_ref[j, row]
        match = lax.rem(tile, modulus) == residue
        for k in range(want):
            hit = match & (seen == k)
            found[k] = jnp.where(hit, tile, found[k])
            places[k] = jnp.where(hit, jnp.int32(j), places[k])
        seen = seen + match.astype(jnp.int32)
    return found, places


def factor_inverse_of(matrix):
    size = matrix.shape[0]
    rows = lax.broadcasted_iota(jnp.int32, matrix.shape, 0)
    cols = lax.broadcasted_iota(jnp.int32, matrix.shape, 1)

    def eliminate(j, carry):
        rest, inverse = carry
        row = jnp.sum(jnp.where(rows == j, rest, 0.0), axis=0, keepdims=True)
        column = jnp.sum(jnp.where(cols == j, rest, 0.0), axis=1, keepdims=True)
        pivot = jnp.sum(jnp.where(cols[:1] == j, row, 0.0), axis=1, keepdims=True)
        scale = 1.0 / jnp.sqrt(pivot)
        below = jnp.where(rows[:, :1] > j, column * scale, 0.0)
        solved = jnp.sum(jnp.where(rows == j, inverse, 0.0), axis=0, keepdims=True) * scale
        rest = rest - below * (row * scale)
        inverse = jnp.where(rows == j, solved, inverse - below * solved)
        return rest, inverse

    return lax.fori_loop(0, size, eliminate, (matrix, (rows == cols).astype(jnp.float32)))[1]


def exchange_kernel(
    layers, layer_rows, cols_grid, rows_per, width,
    tiles_ref, sizes_ref, coupling_ref, factor_ref, base_ref,
    parts_ref, start_ref, side_ref, side_start_ref, inverse_ref, slots_ref,
    block_ref, corner_ref, w_ref, high_ref, low_ref, row_high_ref, row_low_ref, stage_ref, sums_ref, heard_ref,
    load_sem, base_sem, up_send, down_send, arrive, tile_send, tile_recv, side_send, side_recv, share_send, share_recv, sum_send, sum_recv,
):
    classes = layers * layer_rows
    group = layer_rows * cols_grid
    laps = classes // cols_grid
    tile_count = block_ref.shape[0]
    layer, sub, pcol = lax.axis_index("layer"), lax.axis_index("sub"), lax.axis_index("pcol")
    me = sub * cols_grid + pcol
    self_index = layer * group + me
    prow = layer * layer_rows + sub
    last = layers - 1
    block = rows_per * width
    local_cols = base_ref.shape[1]
    share = side_ref.shape[3]

    interior = factor_ref.shape[0]
    side = interior // width

    def factor_tile(n):
        rest, c = divmod(n, rows_per)
        rest, r = divmod(rest, rows_per)
        m, t = divmod(rest, layer_rows)
        return stage_ref.at[1, m, t, r, c]

    def spot(n):
        return slice(n // side * width, (n // side + 1) * width), slice(n % side * width, (n % side + 1) * width)

    loads = [pltpu.make_async_copy(base_ref.at[0, 0], corner_ref, load_sem.at[0])]
    for n in range(side * side):
        loads.append(pltpu.make_async_copy(factor_ref.at[spot(n)], factor_tile(n), load_sem.at[1 + n]))
    for j in range(tile_count):
        tile = coupling_ref.at[:, j * width : (j + 1) * width]
        loads.append(pltpu.make_async_copy(tile, block_ref.at[j], load_sem.at[1 + side * side + j]))
    for load in loads:
        load.start()
    preload = pltpu.make_async_copy(base_ref, start_ref, base_sem)
    preload.start()

    barrier = pltpu.get_barrier_semaphore()

    def greet(k, carry):
        peer = lax.rem(me + k, group)
        pl.semaphore_signal(
            barrier, inc=1, device_id=(layer, peer // cols_grid, lax.rem(peer, cols_grid)), device_id_type=MESH
        )
        return carry

    lax.fori_loop(1, group, greet, 0)
    for other in (last - layer, layer ^ 1):
        pl.semaphore_signal(barrier, inc=1, device_id=(other, sub, pcol), device_id_type=MESH)

    first = jnp.int32(0)
    present = jnp.int32(0)
    for j in range(tile_count):
        hit = tiles_ref[j, self_index] == 0
        first = jnp.where(hit, jnp.int32(j), first)
        present = jnp.where(hit, jnp.int32(1), present)

    for load in loads:
        load.wait()
    for n in range(side * side):
        high, low = split(factor_tile(n)[...])
        row_high_ref[spot(n)] = high
        row_low_ref[spot(n)] = low
    size = sizes_ref[0]

    def weigh(columns, limit):
        live = lax.broadcasted_iota(jnp.int32, columns.shape, 0) < limit
        product = dot3(row_high_ref[:interior], row_low_ref[:interior], *split(jnp.where(live, columns, 0.0)))
        return jnp.where(live, product, 0.0)

    def up_copy(source, m, c):
        return pltpu.make_async_remote_copy(
            src_ref=w_ref.at[source, m, :, c * width : (c + 1) * width],
            dst_ref=w_ref.at[source, m, :, c * width : (c + 1) * width],
            send_sem=up_send.at[source, m, c],
            recv_sem=arrive.at[source, m, c],
            device_id=(jnp.minimum(layer + 1, last), sub, pcol),
            device_id_type=MESH,
        )

    def down_copy(source, m, c):
        return pltpu.make_async_remote_copy(
            src_ref=w_ref.at[source, m, :, c * width : (c + 1) * width],
            dst_ref=w_ref.at[source, m, :, c * width : (c + 1) * width],
            send_sem=down_send.at[source, m, c],
            recv_sem=arrive.at[source, m, c],
            device_id=(jnp.maximum(layer - 1, 0), sub, pcol),
            device_id_type=MESH,
        )

    def pass_up(source, m):
        @pl.when(layer < last)
        def _():
            for c in range(rows_per):
                up_copy(source, m, c).start()

    def pass_down(source, m):
        @pl.when(layer > 0)
        def _():
            for c in range(rows_per):
                down_copy(source, m, c).start()

    steps = sums_ref.shape[0] - 1

    def sum_copy(k):
        if k == 0:
            partner = (last - layer, sub, pcol)
        elif k == 1:
            partner = (layer ^ 1, sub, pcol)
        else:
            peer = me ^ (group >> (k - 1))
            partner = (layer, peer // cols_grid, lax.rem(peer, cols_grid))
        return pltpu.make_async_remote_copy(
            src_ref=sums_ref.at[k],
            dst_ref=heard_ref.at[k],
            send_sem=sum_send.at[k],
            recv_sem=sum_recv.at[k],
            device_id=partner,
            device_id_type=MESH,
        )

    def sum_up(k):
        sum_copy(k).wait()
        sums_ref[k + 1] = sums_ref[k] + heard_ref[k]

    def keep(m, product):
        high, low = split(product)
        high_ref[m] = high
        low_ref[m] = low

    def weigh_class(m):
        order = members(tiles_ref, self_index, tile_count, classes, m, rows_per)[1]
        product = weigh(jnp.concatenate([block_ref[at] for at in order], axis=1), size)
        w_ref[layer, m] = product
        keep(m, product)

    def share_copy(q):
        return pltpu.make_async_remote_copy(
            src_ref=base_ref.at[:, 0, q * share : (q + 1) * share, :],
            dst_ref=side_start_ref,
            send_sem=share_send.at[q],
            recv_sem=share_recv,
            device_id=(layer, sub, q),
            device_id_type=MESH,
        )

    own_share = pltpu.make_async_copy(base_ref.at[:, 0, :share, :], side_start_ref, share_send.at[0])

    middle = classes // 2

    def up_order(i):
        near_end = classes - layer_rows * (1 + i // layer_rows) + lax.rem(i, layer_rows)
        return jnp.where(i < middle, near_end, lax.rem(i + 1 + pcol, middle))

    def down_order(i):
        return jnp.where(i < middle, i, middle + lax.rem(i + 1 + pcol, middle))

    def weigh_pair(i):
        weigh_class(up_order(i))
        weigh_class(down_order(i))

    def pass_pair(i):
        pass_up(layer, up_order(i))
        pass_down(layer, down_order(i))

    weigh_pair(0)
    pl.semaphore_wait(barrier, group + 1)
    pass_pair(0)
    product = weigh(block_ref[first], size * present)
    square = dot3(*split(product.T), *split(product))
    sums_ref[0] = jnp.where(self_index == 0, corner_ref[...], 0.0) - square

    sum_copy(0).start()

    @pl.when(pcol == 0)
    def _():
        own_share.start()
        for q in range(1, cols_grid):
            share_copy(q).start()

    weigh_pair(1)
    pass_pair(1)
    weigh_pair(2)
    sum_up(0)
    sum_copy(1).start()
    pass_pair(2)

    def weigh_rest(i, carry):
        weigh_pair(i)
        return carry

    lax.fori_loop(3, middle, weigh_rest, 0)
    sum_up(1)
    sum_copy(2).start()

    def pass_rest(i, carry):
        pass_pair(i)
        return carry

    lax.fori_loop(3, classes, pass_rest, 0)
    for k in range(2, steps):
        sum_up(k)
        if k + 1 < steps:
            sum_copy(k + 1).start()

    def tiles_out(source, m, slot, target):
        q, lap = lax.rem(m, cols_grid), m // cols_grid
        return pltpu.make_async_remote_copy(
            src_ref=stage_ref.at[slot, m, target],
            dst_ref=parts_ref.at[source * group + me, lap],
            send_sem=tile_send.at[slot, m, target],
            recv_sem=tile_recv.at[source * group + me, lap],
            device_id=(layer, target, q),
            device_id_type=MESH,
        )

    def tile_out(source, m, slot, target, c):
        q, lap = lax.rem(m, cols_grid), m // cols_grid
        return pltpu.make_async_remote_copy(
            src_ref=stage_ref.at[slot, m, target, :, c],
            dst_ref=parts_ref.at[source * group + me, lap, :, c],
            send_sem=tile_send.at[slot, m, target],
            recv_sem=tile_recv.at[source * group + me, lap],
            device_id=(layer, target, q),
            device_id_type=MESH,
        )

    def side_out(source, slot, target, p):
        return pltpu.make_async_remote_copy(
            src_ref=stage_ref.at[slot, 0, target, :, :, pl.ds(p * share, share), :],
            dst_ref=side_ref.at[source * group + me],
            send_sem=side_send.at[slot, target, p],
            recv_sem=side_recv.at[source * group + me],
            device_id=(layer, target, p),
            device_id_type=MESH,
        )

    def take_rows(source):
        for t in range(layer_rows):
            high, low = split(w_ref[source, layer * layer_rows + t].T)
            row_high_ref[t * block : (t + 1) * block] = high
            row_low_ref[t * block : (t + 1) * block] = low

    def column(source, m, slot, picked):
        q, lap = lax.rem(m, cols_grid), m // cols_grid
        span = slice(picked[0] * width, (picked[-1] + 1) * width)
        for t in range(layer_rows):
            rows = slice(t * block, (t + 1) * block)
            product = dot3(row_high_ref[rows], row_low_ref[rows], high_ref[m, :, span], low_ref[m, :, span])
            away = (q != pcol) | (sub != t)

            def write(ref):
                for r in range(rows_per):
                    for n, c in enumerate(picked):
                        ref[r, c] = product[r * width : (r + 1) * width, n * width : (n + 1) * width]

            @pl.when(away | (m == 0))
            def _():
                write(stage_ref.at[slot, m, t])

            @pl.when(away)
            def _():
                if len(picked) == rows_per:
                    tiles_out(source, m, slot, t).start()
                else:
                    for c in picked:
                        tile_out(source, m, slot, t, c).start()

            @pl.when(jnp.logical_not(away))
            def _():
                write(parts_ref.at[source * group + me, lap])

            @pl.when(m == 0)
            def _():
                for p in range(cols_grid):

                    @pl.when((p == pcol) & (sub == t))
                    def _():
                        for r in range(rows_per):
                            for n, c in enumerate(picked):
                                top = r * width + p * share
                                side_ref[source * group + me, r, c] = product[
                                    top : top + share, n * width : (n + 1) * width
                                ]

                    if picked[-1] == rows_per - 1:

                        @pl.when((p != pcol) | (sub != t))
                        def _():
                            side_out(source, slot, t, p).start()

    def sent(source, slot):
        def wait(n, carry):
            m, t = n // layer_rows, lax.rem(n, layer_rows)

            @pl.when((lax.rem(m, cols_grid) != pcol) | (sub != t))
            def _():
                tiles_out(source, m, slot, t).wait_send()

            return carry

        lax.fori_loop(0, classes * layer_rows, wait, 0)
        for t in range(layer_rows):
            for p in range(cols_grid):

                @pl.when((p != pcol) | (sub != t))
                def _():
                    side_out(source, slot, t, p).wait_send()

    def columns(source, slot, ordered, low, top):
        def step(i, carry):
            column(source, ordered(i), slot, tuple(range(rows_per)))
            return carry

        lax.fori_loop(low, top, step, 0)

    def straight(i):
        return i

    take_rows(layer)
    columns(layer, 0, straight, 0, classes)

    total = sums_ref[steps]
    inverse_ref[...] = factor_inverse_of(0.5 * (total + total.T))

    each = rows_per * laps * rows_per

    def place_tiles(sender, carry):
        row_tiles = members(tiles_ref, sender, tile_count, classes, prow, rows_per)[0]
        for lap in range(laps):
            col_tiles = members(tiles_ref, sender, tile_count, classes, lap * cols_grid + pcol, rows_per)[0]
            for r in range(rows_per):
                for c in range(rows_per):
                    slots_ref[sender * each + (lap * rows_per + r) * rows_per + c] = (
                        row_tiles[r] // classes * local_cols + col_tiles[c] // cols_grid
                    )
        zeros = members(tiles_ref, sender, tile_count, classes, 0, rows_per)[0]
        pick = jnp.int32(-1)
        for c in range(rows_per):
            pick = jnp.where(zeros[c] == 0, jnp.int32(c), pick)
        slots_ref[layers * group * each + sender] = pick
        return carry

    def up_onward(source, m, c):
        @pl.when(layer < last)
        def _():
            up_copy(source, m, c).start()

    def down_onward(source, m, c):
        @pl.when(layer > 0)
        def _():
            down_copy(source, m, c).start()

    def relay(i, carry):
        @pl.when(layer > 0)
        def _():
            source, m = layer - 1, up_order(i)
            for c in range(rows_per):
                up_copy(source, m, c).wait_recv()
                up_onward(source, m, c)

        @pl.when(layer < last)
        def _():
            source, m = layer + 1, down_order(i)
            for c in range(rows_per):
                down_copy(source, m, c).wait_recv()
                down_onward(source, m, c)

        return carry

    lax.fori_loop(0, classes, relay, 0)

    def absorb(source, slot):
        def prepare(m, carry):
            keep(m, w_ref[source, m])
            return carry

        lax.fori_loop(0, classes, prepare, 0)
        take_rows(source)
        columns(source, slot, straight, 0, classes)

    @pl.when(layer > 0)
    def _():
        absorb(layer - 1, 1)

    sent(layer, 0)

    @pl.when(layer < last)
    def _():
        absorb(layer + 1, 0)

    @pl.when(layer > 0)
    def _():
        sent(layer - 1, 1)

    rising = layer >= layers // 2

    def order(i):
        return jnp.where(rising, up_order(i), down_order(i))

    def stream(distance, slot, passing):
        source = jnp.where(rising, layer - distance, layer + distance)

        def receive(m, c):
            up_copy(source, m, c).wait_recv()
            if passing:

                @pl.when(rising)
                def _():
                    up_onward(source, m, c)

                @pl.when(jnp.logical_not(rising))
                def _():
                    down_onward(source, m, c)

            half = slice(c * width, (c + 1) * width)
            high, low = split(w_ref[source, m, :, half])
            high_ref[m, :, half] = high
            low_ref[m, :, half] = low

        def gather(i, carry):
            for c in range(rows_per):
                receive(order(i), c)
            return carry

        lax.fori_loop(0, middle, gather, 0)
        take_rows(source)
        columns(source, slot, order, 0, middle)

        def step(i, carry):
            for c in range(rows_per):
                receive(order(i), c)
                column(source, order(i), slot, (c,))
            return carry

        lax.fori_loop(middle, classes, step, 0)

    stream(2, 1, True)
    lax.fori_loop(0, layers * group, place_tiles, 0)

    @pl.when(layer < last)
    def _():
        sent(layer + 1, 0)

    ends = (layer == 0) | (layer == last)

    def landed(source):
        def wait(k, carry):
            peer = lax.rem(me + k, group)
            for lap in range(laps):
                pltpu.make_async_remote_copy(
                    src_ref=stage_ref.at[0, 0, 0],
                    dst_ref=parts_ref.at[source * group + peer, lap],
                    send_sem=tile_send.at[0, 0, 0],
                    recv_sem=tile_recv.at[source * group + peer, lap],
                    device_id=(layer, peer // cols_grid, lax.rem(peer, cols_grid)),
                    device_id_type=MESH,
                ).wait_recv()
            pltpu.make_async_remote_copy(
                src_ref=stage_ref.at[0, 0, 0, :, :, pl.ds(0, share), :],
                dst_ref=side_ref.at[source * group + peer],
                send_sem=side_send.at[0, 0, 0],
                recv_sem=side_recv.at[source * group + peer],
                device_id=(layer, peer // cols_grid, lax.rem(peer, cols_grid)),
                device_id_type=MESH,
            ).wait_recv()

            return carry

        lax.fori_loop(1, group, wait, 0)

    @pl.when(pcol == 0)
    def _():
        own_share.wait()
        for q in range(1, cols_grid):
            share_copy(q).wait_send()

    @pl.when(pcol != 0)
    def _():
        share_copy(1).wait_recv()

    farthest = jnp.where(rising, layer - 3, layer + 3)

    def landed_early(source, carry):
        @pl.when(jnp.logical_not(ends) | (source != farthest))
        def _():
            landed(source)

        return carry

    lax.fori_loop(0, layers, landed_early, 0)
    sent(jnp.where(rising, layer - 2, layer + 2), 1)
    def passed(source, carry):
        def wait(m, inner):
            @pl.when((source <= layer) & (layer < last))
            def _():
                for c in range(rows_per):
                    up_copy(source, m, c).wait_send()

            @pl.when((source >= layer) & (layer > 0))
            def _():
                for c in range(rows_per):
                    down_copy(source, m, c).wait_send()

            return inner

        return lax.fori_loop(0, classes, wait, carry)

    lax.fori_loop(0, layers, passed, 0)
    preload.wait()

    @pl.when(ends)
    def _():
        stream(3, 0, False)
        landed(farthest)
        sent(farthest, 0)


def exchange(tiles, sizes, coupling, factor, base, layers, layer_rows, cols_grid):
    interior, iface = coupling.shape
    width = base.shape[-1]
    classes = layers * layer_rows
    rows_per = iface // width // classes
    laps = classes // cols_grid
    group = layer_rows * cols_grid
    senders = layers * group
    parts = (senders, laps, rows_per, rows_per, width, width)
    chunks = (classes, interior, rows_per * width)
    steps = senders.bit_length() - 1
    share = width // cols_grid
    dma = pltpu.SemaphoreType.DMA
    vmem = pl.BlockSpec(memory_space=pltpu.VMEM)
    hbm = pl.BlockSpec(memory_space=pltpu.HBM)
    scalars = pl.BlockSpec(memory_space=pltpu.SMEM)
    return pl.pallas_call(
        functools.partial(exchange_kernel, layers, layer_rows, cols_grid, rows_per, width),
        in_specs=[scalars, scalars, hbm, hbm, hbm],
        out_specs=[vmem, vmem, vmem, vmem, vmem, scalars],
        out_shape=[
            pltpu.VMEM(parts, jnp.float32),
            pltpu.VMEM(base.shape, jnp.float32),
            pltpu.VMEM((senders, rows_per, rows_per, share, width), jnp.float32),
            pltpu.VMEM((base.shape[0], share, width), jnp.float32),
            pltpu.VMEM((width, width), jnp.float32),
            jax.ShapeDtypeStruct((senders * (laps * rows_per * rows_per + 1),), jnp.int32),
        ],
        scratch_shapes=[
            pltpu.VMEM((iface // width, interior, width), jnp.float32),
            pltpu.VMEM((width, width), jnp.float32),
            pltpu.VMEM((layers, *chunks), jnp.float32),
            pltpu.VMEM(chunks, jnp.bfloat16),
            pltpu.VMEM(chunks, jnp.bfloat16),
            pltpu.VMEM((max(interior, iface // layers), interior), jnp.bfloat16),
            pltpu.VMEM((max(interior, iface // layers), interior), jnp.bfloat16),
            pltpu.VMEM((2, classes, layer_rows, rows_per, rows_per, width, width), jnp.float32),
            pltpu.VMEM((steps + 1, width, width), jnp.float32),
            pltpu.VMEM((steps, width, width), jnp.float32),
            dma((iface // width + (interior // width) ** 2 + 1,)), dma,
            dma((layers, classes, rows_per)), dma((layers, classes, rows_per)), dma((layers, classes, rows_per)),
            dma((2, classes, layer_rows)), dma((senders, laps)),
            dma((2, layer_rows, cols_grid)), dma((senders,)),
            dma((cols_grid,)), dma,
            dma((steps,)), dma((steps,)),
        ],
        compiler_params=pltpu.CompilerParams(
            vmem_limit_bytes=37 << 20, collective_id=0, has_side_effects=True
        ),
        name="exchange",
    )(tiles, sizes, *(pltpu.with_memory_space_constraint(x, pltpu.HBM) for x in (coupling, factor, base)))


def subtract_kernel(
    slots_ref, start_ref, parts_ref, side_ref, side_start_ref, inverse_ref,
    out_ref, panel_ref, sum_ref, column_ref, store_sem,
):
    senders, count = parts_ref.shape[:2]
    local_cols, rows_per = out_ref.shape[0] // side_start_ref.shape[0], side_ref.shape[1]

    def take(n, carry):
        for i in range(count):
            slot = slots_ref[n * count + i]
            sum_ref[slot] = sum_ref[slot] - parts_ref[n, i]
        return carry

    lax.fori_loop(0, senders, take, 0)
    store = pltpu.make_async_copy(sum_ref, out_ref, store_sem.at[0])
    store.start()
    column_ref[...] = side_start_ref[...]

    def pick(n, carry):
        chosen = slots_ref[senders * count + n]

        @pl.when(chosen >= 0)
        def _():
            for r in range(rows_per):
                slot = slots_ref[n * count + r * rows_per] // local_cols
                column_ref[slot] = column_ref[slot] - side_ref[n, r, chosen]

        return carry

    lax.fori_loop(0, senders, pick, 0)
    column = column_ref[...].reshape(-1, column_ref.shape[-1])
    panel = jnp.dot(column, inverse_ref[...].T, precision=HIGHEST, preferred_element_type=jnp.float32)
    column_ref[...] = panel.reshape(column_ref.shape)
    ready = pltpu.make_async_copy(column_ref, panel_ref, store_sem.at[1])
    ready.start()
    store.wait()
    ready.wait()


def subtract(slots, start, parts, side, side_start, inverse):
    vmem = pl.BlockSpec(memory_space=pltpu.VMEM)
    hbm = pl.BlockSpec(memory_space=pltpu.HBM)
    return pl.pallas_call(
        subtract_kernel,
        in_specs=[pl.BlockSpec(memory_space=pltpu.SMEM), vmem, vmem, vmem, vmem, vmem],
        out_specs=[hbm, hbm, vmem],
        out_shape=[
            pltpu.HBM(start.shape, jnp.float32),
            pltpu.HBM(side_start.shape, jnp.float32),
            pltpu.VMEM(start.shape, jnp.float32),
        ],
        input_output_aliases={1: 2},
        scratch_shapes=[pltpu.VMEM(side_start.shape, jnp.float32), pltpu.SemaphoreType.DMA((2,))],
        compiler_params=pltpu.CompilerParams(vmem_limit_bytes=2 << 20),
        cost_estimate=pl.CostEstimate(
            flops=parts.size, bytes_accessed=8 * parts.size + 4 * start.size, transcendentals=0
        ),
        name="subtract",
    )(slots, start, parts, side, side_start, inverse)


def shards(iface_tiles, interior_sizes, coupling, factor_inverse, interface_block):
    layers, layer_rows = lax.axis_size("layer"), lax.axis_size("sub")
    cols_grid = lax.axis_size("pcol")
    width = interface_block.shape[-1]
    base = interface_block[0, :, 0]
    parts, start, side, side_start, inverse, slots = exchange(
        iface_tiles.T, interior_sizes, coupling[0], factor_inverse[0], base, layers, layer_rows, cols_grid
    )
    summed, panel, _ = subtract(
        slots,
        start.reshape(-1, width, width),
        parts.reshape(parts.shape[0], -1, width, width),
        side,
        side_start,
        inverse,
    )
    return (summed.reshape(interface_block.shape), panel[None])


def solution(mesh):
    rows_grid, cols_grid = mesh.shape["prow"], mesh.shape["pcol"]
    grid = Mesh(
        mesh.devices.reshape(LAYERS, rows_grid // LAYERS, cols_grid), ("layer", "sub", "pcol")
    )
    prow = ("layer", "sub")
    every = ("layer", "sub", "pcol")
    in_specs = (
        P(),
        P(every),
        P(every, None, None),
        P(every, None, None),
        P(prow, None, "pcol", None, None, None),
    )
    out_specs = (P(prow, None, "pcol", None, None, None), P(prow, None, "pcol", None))
    return jax.shard_map(shards, mesh=grid, in_specs=in_specs, out_specs=out_specs, check_vma=False)
```

time: 314 us -> 303 us (0.965)
  waiting for transfers between devices: 7.53 us -> 0 us
    ppermute x3 -> x0, waiting for transfers between devices: 7.53 us -> none  [shards(): lax.ppermute(column[:, q * share:(q + 1) * share], 'pcol', [(0, q)])]
  transfers between devices with their start and end apart: 3 -> 0, of which waited for: 1 -> 0; matrix products, arithmetic and copies ran while one was open for 0% -> 0% of each run, Pallas kernels for 0% -> 0%
where the time goes in v2:
time: 303 us; the launch traced here: 300 us
  Pallas kernels  298 us (98%)
    pallas_call x1, Pallas kernels, exchange(): pl.pallas_call(functools.partial(exchange_kernel, layers, layer_rows, col...  292 us

profile of v2, /device:TPU:7, one launch (start us, length us, event | category | flops | bytes accessed | tf_op | source)
XLA Modules:
  0.0 300.1 jit_solution(16706196485442506172)
XLA Ops:
  1.3 291.9 %exchange.1 = (f32[32,2,2,2,128,128]{5,4,3,2,1,0:T(8,128)S(1)}, f32[8,16,128,128]{3,2,1,0:T(8,128)S(1)}, f32[32,2,2,32,128]{4,3,2,1,0:T(8,128)S(1)}, f32[8,32,12...) custom-call(s32[16,32]{1,0:T(8,128)} %bitcast.15, s32[1]{0:T(128)S(6)} %copy.10.sizes_ref, ...), custom_call_target="tpu_custom_call" | custom-call | tf_op jit(solution)/shard_map/exchange/pallas_call | solution.py:600
  293.2 0.0 copy-start
  293.2 0.7 copy-done
  293.9 6.0 %subtract.1 = (f32[128,128,128]{2,1,0:T(8,128)}, f32[8,32,128]{2,1,0:T(8,128)}, f32[128,128,128]{2,1,0:T(8,128)S(1)}) custom-call(s32[288]{0:T(512)S(1)} %copy-done, f32[128,128,128]{2,1,0:T(8,128)S(1)} %bitcast.11, f32[32,8,128,128]{3,2,1,0:T(8,128)S(1)} %bitcast.10, ...), custom_call_target="tpu_custom_call", output_to_operand_aliasing={{2}: (1, {})} | custom-call | flops 4194304 | bytes 41943040 | tf_op jit(solution)/shard_map/subtract/pallas_call | solution.py:679
Async XLA Ops:
  293.2 0.7 copy-start

commit v3 on v2

--- a/solution.py
+++ b/solution.py
@@ -98,7 +98,6 @@
     for load in loads:
         load.start()
     preload = pltpu.make_async_copy(base_ref, start_ref, base_sem)
-    preload.start()
 
     barrier = pltpu.get_barrier_semaphore()
 
@@ -231,6 +230,7 @@
     weigh_pair(0)
     pl.semaphore_wait(barrier, group + 1)
     pass_pair(0)
+    preload.start()
     product = weigh(block_ref[first], size * present)
     square = dot3(*split(product.T), *split(product))
     sums_ref[0] = jnp.where(self_index == 0, corner_ref[...], 0.0) - square
@@ -463,20 +463,51 @@
     def order(i):
         return jnp.where(rising, up_order(i), down_order(i))
 
+    near = jnp.where(rising, layer - 1, layer + 1)
+    second = jnp.where(rising, layer - 2, layer + 2)
+    final = order(classes - 1)
+
     def stream(distance, slot, passing):
         source = jnp.where(rising, layer - distance, layer + distance)
 
-        def receive(m, c):
+        if passing:
+
+            def settle(m, carry):
+                for c in range(rows_per):
+
+                    @pl.when(rising & (layer < last))
+                    def _():
+                        up_copy(near, m, c).wait_send()
+
+                    @pl.when(jnp.logical_not(rising) & (layer > 0))
+                    def _():
+                        down_copy(near, m, c).wait_send()
+
+                return carry
+
+            lax.fori_loop(0, classes, settle, 0)
+
+        def receive(i, c):
+            m = order(i)
             up_copy(source, m, c).wait_recv()
             if passing:
-
-                @pl.when(rising)
+                before = order(jnp.maximum(i - 1, 0))
+
+                @pl.when(rising & (layer < last))
                 def _():
-                    up_onward(source, m, c)
-
-                @pl.when(jnp.logical_not(rising))
+                    @pl.when(i > 0)
+                    def _():
+                        up_copy(source, before, c).wait_send()
+
+                    up_copy(source, m, c).start()
+
+                @pl.when(jnp.logical_not(rising) & (layer > 0))
                 def _():
-                    down_onward(source, m, c)
+                    @pl.when(i > 0)
+                    def _():
+                        down_copy(source, before, c).wait_send()
+
+                    down_copy(source, m, c).start()
 
             half = slice(c * width, (c + 1) * width)
             high, low = split(w_ref[source, m, :, half])
@@ -485,7 +516,7 @@
 
         def gather(i, carry):
             for c in range(rows_per):
-                receive(order(i), c)
+                receive(i, c)
             return carry
 
         lax.fori_loop(0, middle, gather, 0)
@@ -494,7 +525,7 @@
 
         def step(i, carry):
             for c in range(rows_per):
-                receive(order(i), c)
+                receive(i, c)
                 column(source, order(i), slot, (c,))
             return carry
 
@@ -557,12 +588,14 @@
     sent(jnp.where(rising, layer - 2, layer + 2), 1)
     def passed(source, carry):
         def wait(m, inner):
-            @pl.when((source <= layer) & (layer < last))
+            kept = (source != near) & ((source != second) | (m == final))
+
+            @pl.when((source <= layer) & (layer < last) & kept)
             def _():
                 for c in range(rows_per):
                     up_copy(source, m, c).wait_send()
 
-            @pl.when((source >= layer) & (layer > 0))
+            @pl.when((source >= layer) & (layer > 0) & kept)
             def _():
                 for c in range(rows_per):
                     down_copy(source, m, c).wait_send()
@@ -607,7 +640,7 @@
             pltpu.VMEM((senders, rows_per, rows_per, share, width), jnp.float32),
             pltpu.VMEM((base.shape[0], share, width), jnp.float32),
             pltpu.VMEM((width, width), jnp.float32),
-            jax.ShapeDtypeStruct((senders * (laps * rows_per * rows_per + 1),), jnp.int32),
+            pltpu.SMEM((senders * (laps * rows_per * rows_per + 1),), jnp.int32),
         ],
         scratch_shapes=[
             pltpu.VMEM((iface // width, interior, width), jnp.float32),
@@ -648,8 +681,12 @@
         return carry
 
     lax.fori_loop(0, senders, take, 0)
-    store = pltpu.make_async_copy(sum_ref, out_ref, store_sem.at[0])
-    store.start()
+    local_rows = side_start_ref.shape[0]
+    stores = []
+    for a in range(local_rows):
+        tiles = pl.ds(a * local_cols, local_cols)
+        stores.append(pltpu.make_async_copy(sum_ref.at[tiles], out_ref.at[tiles], store_sem.at[1 + a]))
+        stores[-1].start()
     column_ref[...] = side_start_ref[...]
 
     def pick(n, carry):
@@ -667,9 +704,10 @@
     column = column_ref[...].reshape(-1, column_ref.shape[-1])
     panel = jnp.dot(column, inverse_ref[...].T, precision=HIGHEST, preferred_element_type=jnp.float32)
     column_ref[...] = panel.reshape(column_ref.shape)
-    ready = pltpu.make_async_copy(column_ref, panel_ref, store_sem.at[1])
+    ready = pltpu.make_async_copy(column_ref, panel_ref, store_sem.at[0])
     ready.start()
-    store.wait()
+    for store in stores:
+        store.wait()
     ready.wait()
 
 
@@ -686,7 +724,7 @@
             pltpu.VMEM(start.shape, jnp.float32),
         ],
         input_output_aliases={1: 2},
-        scratch_shapes=[pltpu.VMEM(side_start.shape, jnp.float32), pltpu.SemaphoreType.DMA((2,))],
+        scratch_shapes=[pltpu.VMEM(side_start.shape, jnp.float32), pltpu.SemaphoreType.DMA((1 + side_start.shape[0],))],
         compiler_params=pltpu.CompilerParams(vmem_limit_bytes=2 << 20),
         cost_estimate=pl.CostEstimate(
             flops=parts.size, bytes_accessed=8 * parts.size + 4 * start.size, transcendentals=0

time: 303 us -> 301 us (level)
  no operation moved by 1% of the time
where the time goes in v3:
time: 301 us; the launch traced here: 298 us
  Pallas kernels  296 us (98%)
    pallas_call x1, Pallas kernels, exchange(): pl.pallas_call(functools.partial(exchange_kernel, layers, layer_rows, col...  291 us

profile of v3, /device:TPU:7, one launch (start us, length us, event | category | flops | bytes accessed | tf_op | source)
XLA Modules:
  0.0 297.8 jit_solution(8699133415655475454)
XLA Ops:
  1.3 290.7 %exchange.1 = (f32[32,2,2,2,128,128]{5,4,3,2,1,0:T(8,128)S(1)}, f32[8,16,128,128]{3,2,1,0:T(8,128)S(1)}, f32[32,2,2,32,128]{4,3,2,1,0:T(8,128)S(1)}, f32[8,32,12...) custom-call(s32[16,32]{1,0:T(8,128)} %bitcast.15, s32[1]{0:T(128)S(6)} %copy.10.sizes_ref, ...), custom_call_target="tpu_custom_call" | custom-call | tf_op jit(solution)/shard_map/exchange/pallas_call | solution.py:633
  292.0 5.7 %subtract.1 = (f32[128,128,128]{2,1,0:T(8,128)}, f32[8,32,128]{2,1,0:T(8,128)}, f32[128,128,128]{2,1,0:T(8,128)S(1)}) custom-call(s32[288]{0:T(512)S(4)} %get-tuple-element.10.slots_ref, f32[128,128,128]{2,1,0:T(8,128)S(1)} %bitcast.11, f32[32,8,128,128]{3,2,1,0:T(8,128)S(1)} %bitcast.10, ...), custom_call_target="tpu_custom_call", output_to_operand_aliasing={{2}: (1, {})} | custom-call | flops 4194304 | bytes 41943040 | tf_op jit(solution)/shard_map/subtract/pallas_call | solution.py:717
